TPU v7x, 256 devices: a whole 4x4x8 slice. The times are simulated.
256 devices in a mesh: param: 32 (over z, x), task: 8 (over y, core).
Axes of the slice: x: 4, y: 4, z: 8, core: 2. Of those that a mesh axis runs over, the one named last changes fastest.
Arguments:
- task_ids: int32 [1024], P('task'), may hold values from 0 to 2047
- task_table: bfloat16 [2048, 256], P('param'), may hold values from -12 to 12
- enc_in: bfloat16 [256, 512], replicated, may hold values from -0.375 to 0.375
- enc_out: bfloat16 [512, 256], replicated, may hold values from -0.25 to 0.25
- generator: bfloat16 [256, 8, 114688], P(None, None, ('param', 'task')), may hold values from -6 to 6
- gain: bfloat16 [8, 114688], P(None, ('param', 'task')), may hold values from 0.099609375 to 1.8984375
Outputs:
- adapters: bfloat16 [1024, 8, 114688], P(None, None, ('param', 'task'))
Inputs may be any that keep to these rules, and one draw needn't show every extreme that they name: `task_ids`: each id names a row of task_table.
All inputs are finite; a program needn't handle non-finite values.
Results may differ from a plain program's by a relative error of at most 0.00055.
The roundings to bfloat16 on the way count: a program that leaves them out, or rounds other values in their place, can miss the bound.
Values may be sent and summed in bfloat16 or wider, within the bound.
No kernel may reach another device: no remote copies, remote signals or barrier semaphores. Data moves between devices by JAX's collectives and lax.ppermute only.
A program may use at most 64 MiB of HBM per device.

v0:
```python
import jax
import jax.numpy as jnp
from jax import lax
from jax.sharding import Mesh
from jax.sharding import PartitionSpec as P

D = 3584
RANK = 32
PARAM = ("param_0", "param_1")
TASK = ("task_0", "task_1")
PARAM_TASK = ("param_0", "param_1", "task_0", "task_1")
EPSILON = 1e-06


def laid_out(tiles, dim):
    lengths = list(tiles.shape[1:])
    lengths[dim] *= tiles.shape[0]
    return jnp.moveaxis(tiles, 0, dim).reshape(lengths)


def copy_for_each(x, axis):
    copies = jnp.broadcast_to(x, (lax.axis_size(axis), *x.shape))
    return lax.all_to_all(copies, axis, split_axis=0, concat_axis=0, tiled=True)


def gathered_copies(x, axis, dim):
    return laid_out(copy_for_each(x, axis), dim)


def over_copies(x, axis):
    return copy_for_each(x, axis).sum(axis=0)


def by_axis(x, axes):
    far, near = axes
    return over_copies(over_copies(x, near), far)


def select_rows(wanted, table_part):
    labels = lax.broadcasted_iota(jnp.int32, (1, table_part.shape[0]), 1)
    one_hot = (wanted[:, None] == labels).astype(jnp.bfloat16)
    return jnp.dot(one_hot, table_part, preferred_element_type=jnp.float32)


def look_up(wanted, task_table):
    whole_table = gathered_copies(task_table, PARAM, 0)
    found = select_rows(wanted, whole_table).astype(jnp.bfloat16)
    return found


def encode(raw_rows, enc_in, enc_out):
    inner_act = jax.nn.gelu(jnp.dot(raw_rows, enc_in, preferred_element_type=jnp.float32)).astype(
        jnp.bfloat16
    )
    mixed_sum = raw_rows.astype(jnp.float32) + jnp.dot(
        inner_act, enc_out, preferred_element_type=jnp.float32
    )
    return mixed_sum.astype(jnp.bfloat16)


def on_device(task_ids, task_table, enc_in, enc_out, generator, gain):
    groups = generator.shape[1]
    columns = generator.shape[2]
    flat_weights = generator.reshape(generator.shape[0], groups * columns)
    every_id = lax.all_gather(task_ids, TASK, axis=0, tiled=True)
    embedded = encode(look_up(every_id, task_table), enc_in, enc_out)
    generated = jnp.dot(embedded, flat_weights, preferred_element_type=jnp.float32)
    generated = generated.reshape(generated.shape[0], groups, columns)
    squares = jnp.sum(generated * generated, axis=2)
    totals = by_axis(squares, ("param_0", ("param_1", "task_0", "task_1")))
    inverse = lax.rsqrt(totals / (D * RANK) + EPSILON)
    scaled = generated * inverse[:, :, None] * gain.astype(jnp.float32)[None, :, :]
    return scaled.astype(jnp.bfloat16)


def solution(mesh):
    torus = Mesh(mesh.devices.reshape(8, 4, 4, 2), ("param_0", "param_1", "task_0", "task_1"))
    return jax.shard_map(
        on_device,
        mesh=torus,
        in_specs=(
            P(TASK),
            P(PARAM, None),
            P(),
            P(),
            P(None, None, PARAM_TASK),
            P(None, PARAM_TASK),
        ),
        out_specs=P(None, None, PARAM_TASK),
        check_vma=False,
    )
```

profile of v0, /device:TPU:1, one launch (start us, length us, event | category | flops | bytes accessed | tf_op | source)
XLA Modules:
  0.0 105.5 jit_solution(1677882748042664104)
XLA Ops:
  0.0 0.0 copy-start
  0.0 0.0 copy-start.2
  0.0 2.0 %broadcast_in_dim.12 = bf16[32,64,256]{2,1,0:T(8,128)(2,1)} broadcast(bf16[64,256]{1,0:T(8,128)(2,1)} %param.7), dimensions={1,2} | broadcast | bytes 1081344 | tf_op jit(solution)/shard_map/broadcast_in_dim | solution.py:22
  2.0 11.9 %all-to-all-start = ((bf16[32,64,256]{2,1,0:T(8,128)(2,1)}), bf16[32,64,256]{2,1,0:T(8,128)(2,1)S(1)}, u32[]{:S(2)}, u32[]{:S(2)}) async-start(bf16[32,64,256]{2,1,0:T(8,128)(2,1)} %broadcast_in_dim.12), calls=%async_computation | async-start | bytes 2097152 | tf_op jit(solution)/shard_map/all_to_all | solution.py:23
  13.9 0.0 copy-done.2
  13.9 11.6 %all-gather = s32[8,1,128]{2,1,0:T(1,128)S(1)} all-gather(s32[1,1,128]{2,1,0:T(1,128)S(1)} %bitcast.21), channel_id=1, replica_groups=mesh['param_0'=8,'param_1'=4,'task_0'=4,'task_1'=2] {'task_0','task_1'}, dimensions={0}, use_global_device_ids=true | all-gather | bytes 4608 | tf_op jit(solution)/shard_map/all_gather | solution.py:65
  25.5 14.6 %all-to-all-done = bf16[32,64,256]{2,1,0:T(8,128)(2,1)S(1)} async-done(((bf16[32,64,256]{2,1,0:T(8,128)(2,1)}), bf16[32,64,256]{2,1,0:T(8,128)(2,1)S(1)}, u32[]{:S(2)}, u32[]{:S(2)}) %all-to-all-start) | async-done | bytes 1048608 | tf_op jit(solution)/shard_map/all_to_all | solution.py:23
  40.1 0.0 copy-start.3
  40.1 0.0 copy-start.4
  40.1 2.3 %fusion.15 = bf16[1024,256]{1,0:T(8,128)(2,1)} fusion(bf16[2048,256]{1,0:T(8,128)(2,1)S(1)} %bitcast.19, s32[1024]{0:T(1024)S(1)} %bitcast.20), kind=kOutput, calls=%fused_computation.19 | convolution fusion | flops 1076101120 | bytes 1576960 | tf_op jit(solution)/shard_map/dot_general | solution.py:42
  42.4 0.0 copy-done.3
  42.4 0.0 copy-done.4
  42.4 2.2 %fusion.16 = bf16[1024,256,1]{1,0,2:T(8,128)(2,1)S(1)} fusion(bf16[512,256]{1,0:T(8,128)(2,1)S(1)} %copy-done.3, bf16[1024,256]{1,0:T(8,128)(2,1)} %fusion.15, bf16[256,512]{1,0:T(8,128)(2,1)S(1)} %copy-done.4), kind=kOutput, calls=%fused_computation.20 | convolution fusion | flops 542375936 | bytes 1572864 | tf_op jit(solution)/shard_map/dot_general | solution.py:55
  44.6 0.0 copy-done
  44.6 7.3 %multiply_reduce_fusion = (f32[1024,8]{0,1:T(8,128)S(1)}, f32[1024,8,448]{0,2,1:T(8,128)}) fusion(bf16[1024,256,1]{1,0,2:T(8,128)(2,1)S(1)} %fusion.16, bf16[256,8,448]{0,2,1:T(8,128)(2,1)S(1)} %copy-done), kind=kOutput, calls=%fused_computation.1 | convolution fusion | flops 1886380032 | bytes 17072128 | tf_op jit(solution)/shard_map/dot_general | solution.py:67
  51.9 0.1 broadcast_in_dim.13
  52.0 0.0 copy-start.1
  52.1 26.9 %all_to_all.15 = f32[32,1024,8]{1,2,0:T(8,128)S(1)} all-to-all(f32[32,1024,8]{1,2,0:T(8,128)S(1)} %broadcast_in_dim.13), channel_id=1, replica_groups=mesh['param_0'=8,'param_1'=4,'task_0'=4,'task_1'=2] {'param_1','task_0',..., dimensions={0} | all-to-all | bytes 2097152 | tf_op jit(solution)/shard_map/all_to_all | solution.py:23
  79.0 0.1 reduce_sum.28
  79.0 0.7 broadcast_in_dim.14
  79.7 3.4 %all-to-all-start.2 = ((f32[8,1024,8]{1,2,0:T(8,128)}), f32[8,1024,8]{1,2,0:T(8,128)S(1)}, u32[]{:S(2)}, u32[]{:S(2)}) async-start(f32[8,1024,8]{1,2,0:T(8,128)} %broadcast_in_dim.14), calls=%async_computation.2 | async-start | bytes 524288 | tf_op jit(solution)/shard_map/all_to_all | solution.py:23
  83.2 0.0 copy-done.1
  83.2 12.3 %all-to-all-done.2 = f32[8,1024,8]{1,2,0:T(8,128)S(1)} async-done(((f32[8,1024,8]{1,2,0:T(8,128)}), f32[8,1024,8]{1,2,0:T(8,128)S(1)}, u32[]{:S(2)}, u32[]{:S(2)}) %all-to-all-start.2) | async-done | bytes 262176 | tf_op jit(solution)/shard_map/all_to_all | solution.py:23
  95.5 10.0 %multiply_convert_fusion = bf16[1024,8,448]{0,2,1:T(8,128)(2,1)} fusion(f32[1024,8,448]{0,2,1:T(8,128)} %get-tuple-element.6, f32[8,448]{1,0:T(8,128)S(1)} %convert_element_type.23, f32[1024,8]{0,1:T(8,128)S(1)} %add_rsqrt_fusion), kind=kLoop, calls=%fused_computation | loop fusion | flops 11010048 | bytes 22067200 | tf_op jit(solution)/shard_map/convert_element_type | solution.py:73
  (3 shorter events, 0.0 us)
Async XLA Ops:
  0.0 44.6 %copy-start = (bf16[256,8,448]{0,2,1:T(8,128)(2,1)S(1)}, bf16[256,8,448]{0,2,1:T(8,128)(2,1)}, u32[]{:S(2)}) copy-start(bf16[256,8,448]{0,2,1:T(8,128)(2,1)} %param.10) | copy-start | bytes 5505028
  0.0 13.9 %copy-start.2 = (s32[128]{0:T(128)S(1)}, s32[128]{0:T(128)}, u32[]{:S(2)}) copy-start(s32[128]{0:T(128)} %param.6) | copy-start | bytes 1540
  2.0 38.1 %all-to-all-start = ((bf16[32,64,256]{2,1,0:T(8,128)(2,1)}), bf16[32,64,256]{2,1,0:T(8,128)(2,1)S(1)}, u32[]{:S(2)}, u32[]{:S(2)}) async-start(bf16[32,64,256]{2,1,0:T(8,128)(2,1)} %broadcast_in_dim.12), calls=%async_computation | async-start | bytes 2097152 | tf_op jit(solution)/shard_map/all_to_all | solution.py:23
  40.1 2.3 %copy-start.3 = (bf16[512,256]{1,0:T(8,128)(2,1)S(1)}, bf16[512,256]{1,0:T(8,128)(2,1)}, u32[]{:S(2)}) copy-start(bf16[512,256]{1,0:T(8,128)(2,1)} %param.9) | copy-start | bytes 786436
  40.1 2.3 %copy-start.4 = (bf16[256,512]{1,0:T(8,128)(2,1)S(1)}, bf16[256,512]{1,0:T(8,128)(2,1)}, u32[]{:S(2)}) copy-start(bf16[256,512]{1,0:T(8,128)(2,1)} %param.8) | copy-start | bytes 786436
  52.0 31.1 %copy-start.1 = (bf16[8,448]{1,0:T(8,128)(2,1)S(1)}, bf16[8,448]{1,0:T(8,128)(2,1)}, u32[]{:S(2)}) copy-start(bf16[8,448]{1,0:T(8,128)(2,1)} %param.11) | copy-start | bytes 21508
  79.7 15.7 %all-to-all-start.2 = ((f32[8,1024,8]{1,2,0:T(8,128)}), f32[8,1024,8]{1,2,0:T(8,128)S(1)}, u32[]{:S(2)}, u32[]{:S(2)}) async-start(f32[8,1024,8]{1,2,0:T(8,128)} %broadcast_in_dim.14), calls=%async_computation.2 | async-start | bytes 524288 | tf_op jit(solution)/shard_map/all_to_all | solution.py:23
where the time goes:
time: 106 us
  blocking collectives  38.5 us (36%)
  waiting for transfers between devices  26.9 us (25%)
  starting transfers between devices  15.3 us (14%)
  matrix products  11.9 us (11%)
  other arithmetic  10.1 us (10%)
  local copies, waits for them, and re-layouts  2.84 us (3%)
    all_to_all x1, blocking collectives, copy_for_each(): return lax.all_to_all(copies, axis, split_axis=0, concat_axis=0, tiled=True)  26.9 us
    all_to_all x2, waiting for transfers between devices, copy_for_each(): return lax.all_to_all(copies, axis, split_axis=0, concat_axis=0, tiled=True)  26.9 us
    all_to_all x2, starting transfers between devices, copy_for_each(): return lax.all_to_all(copies, axis, split_axis=0, concat_axis=0, tiled=True)  15.3 us
    all_gather x1, blocking collectives, on_device(): every_id = lax.all_gather(task_ids, TASK, axis=0, tiled=True)  11.6 us
    convert_element_type x1, other arithmetic, on_device(): return scaled.astype(jnp.bfloat16)  10 us
    dot_general x1, matrix products, on_device(): jnp.dot(embedded, flat_weights, preferred_element_type=jnp.float32)  7.32 us
    broadcast_in_dim x3, local copies, waits for them, and re-layouts, copy_for_each(): copies = jnp.broadcast_to(x, (lax.axis_size(axis), *x.shape))  2.82 us
    dot_general x1, matrix products, select_rows(): return jnp.dot(one_hot, table_part, preferred_element_type=jnp.float32)  2.3 us
  transfers between devices with their start and end apart: 2, of which 2 were waited for; matrix products, arithmetic and copies ran while one was open for 0% of the time, Pallas kernels for 0%

commit v1 on v0

--- a/solution.py
+++ b/solution.py
@@ -62,7 +62,16 @@
     groups = generator.shape[1]
     columns = generator.shape[2]
     flat_weights = generator.reshape(generator.shape[0], groups * columns)
-    every_id = lax.all_gather(task_ids, TASK, axis=0, tiled=True)
+    refer_sums_all = lambda sheet: jnp.concatenate(
+        jax.lax.all_to_all(
+            jnp.stack([sheet] * jax.lax.psum(1, axis_name=TASK)),
+            axis_name=TASK,
+            split_axis=0,
+            concat_axis=0,
+        ),
+        axis=0,
+    )
+    every_id = refer_sums_all(task_ids)
     embedded = encode(look_up(every_id, task_table), enc_in, enc_out)
     generated = jnp.dot(embedded, flat_weights, preferred_element_type=jnp.float32)
     generated = generated.reshape(generated.shape[0], groups, columns)

time: 106 us -> 111 us (1.047)
  blocking collectives: 38.5 us -> 72.2 us
  waiting for transfers between devices: 26.9 us -> 12.3 us
  starting transfers between devices: 15.3 us -> 3.41 us
  matrix products: 11.9 us -> 9.81 us
    all_to_all x1 -> x2, blocking collectives: 26.9 us -> 61.9 us  [copy_for_each(): return lax.all_to_all(copies, axis, split_axis=0, concat_axis=0, tiled=True)]
    all_to_all x2 -> x1, waiting for transfers between devices: 26.9 us -> 12.3 us  [copy_for_each(): return lax.all_to_all(copies, axis, split_axis=0, concat_axis=0, tiled=True)]
    all_to_all x2 -> x1, starting transfers between devices: 15.3 us -> 3.41 us  [copy_for_each(): return lax.all_to_all(copies, axis, split_axis=0, concat_axis=0, tiled=True)]
    all_gather x1 -> x0, blocking collectives: 11.6 us -> none  [on_device(): every_id = lax.all_gather(task_ids, TASK, axis=0, tiled=True)]
    all_to_all x0 -> x1, blocking collectives: none -> 10.3 us  [on_device(): jax.lax.all_to_all(jnp.stack([sheet] * jax.lax.psum(1, axis_name=TASK)),...]
    dot_general x1, matrix products: 2.23 us -> 0.97 us  [encode(): jnp.dot(inner_act, enc_out, preferred_element_type=jnp.float32)]
    broadcast_in_dim x3, local copies, waits for them, and re-layouts: 2.82 us -> 1.69 us  [copy_for_each(): copies = jnp.broadcast_to(x, (lax.axis_size(axis), *x.shape))]
  transfers between devices with their start and end apart: 2 -> 1, of which waited for: 2 -> 1; matrix products, arithmetic and copies ran while one was open for 0% -> 0% of each run, Pallas kernels for 0% -> 0%
where the time goes in v1:
time: 111 us; the launch traced here: 110 us
  blocking collectives  72.2 us (65%)
  waiting for transfers between devices  12.3 us (11%)
  other arithmetic  9.82 us (9%)
  matrix products  9.81 us (9%)
  starting transfers between devices  3.41 us (3%)
  local copies, waits for them, and re-layouts  2.5 us (2%)
    all_to_all x2, blocking collectives, copy_for_each(): return lax.all_to_all(copies, axis, split_axis=0, concat_axis=0, tiled=True)  61.9 us
    all_to_all x1, waiting for transfers between devices, copy_for_each(): return lax.all_to_all(copies, axis, split_axis=0, concat_axis=0, tiled=True)  12.3 us
    all_to_all x1, blocking collectives, on_device(): jax.lax.all_to_all(jnp.stack([sheet] * jax.lax.psum(1, axis_name=TASK)),...  10.3 us
    convert_element_type x1, other arithmetic, on_device(): return scaled.astype(jnp.bfloat16)  9.71 us
    dot_general x1, matrix products, on_device(): jnp.dot(embedded, flat_weights, preferred_element_type=jnp.float32)  7.34 us
    all_to_all x1, starting transfers between devices, copy_for_each(): return lax.all_to_all(copies, axis, split_axis=0, concat_axis=0, tiled=True)  3.41 us
  transfers between devices with their start and end apart: 1, of which 1 were waited for; matrix products, arithmetic and copies ran while one was open for 0% of the time, Pallas kernels for 0%

profile of v1, /device:TPU:1, one launch (start us, length us, event | category | flops | bytes accessed | tf_op | source)
XLA Modules:
  0.0 110.2 jit_solution(14558475522826182364)
XLA Ops:
  0.0 0.0 copy-start
  0.0 0.8 stack.2
  0.8 10.3 %all_to_all.21 = s32[8,1,128]{2,1,0:T(1,128)S(1)} all-to-all(s32[8,1,128]{2,1,0:T(1,128)S(1)} %stack.2), channel_id=1, replica_groups=mesh['param_0'=8,'param_1'=4,'task_0'=4,'task_1'=2] {'task_0','task_1'}, dimensions={0} | all-to-all | bytes 8192 | tf_op jit(solution)/shard_map/all_to_all | solution.py:66
  11.1 0.9 broadcast_in_dim.11
  12.0 37.0 %all_to_all.22 = bf16[32,64,256]{2,1,0:T(8,128)(2,1)S(1)} all-to-all(bf16[32,64,256]{2,1,0:T(8,128)(2,1)S(1)} %broadcast_in_dim.11), channel_id=1, replica_groups=mesh['param_0'=8,'param_1'=4,'task_0'=4,'task_1'=2] {'param_0','param_1'}, dimensions={0} | all-to-all | bytes 2097152 | tf_op jit(solution)/shard_map/all_to_all | solution.py:23
  49.0 0.0 copy-start.2
  49.0 0.0 copy-start.3
  49.0 1.5 %fusion.15 = bf16[1024,256]{1,0:T(8,128)(2,1)S(1)} fusion(bf16[2048,256]{1,0:T(8,128)(2,1)S(1)} %bitcast.18, s32[1024]{0:T(1024)S(1)} %bitcast.19), kind=kOutput, calls=%fused_computation.19 | convolution fusion | flops 1076101120 | bytes 1576960 | tf_op jit(solution)/shard_map/dot_general | solution.py:42
  50.6 0.0 copy-done.2
  50.6 0.0 copy-done.3
  50.6 1.0 fusion.16
  51.6 0.0 copy-done
  51.6 7.3 %multiply_reduce_fusion = (f32[1024,8]{0,1:T(8,128)S(1)}, f32[1024,8,448]{0,2,1:T(8,128)}) fusion(bf16[1024,256,1]{1,0,2:T(8,128)(2,1)S(1)} %fusion.16, bf16[256,8,448]{0,2,1:T(8,128)(2,1)S(1)} %copy-done), kind=kOutput, calls=%fused_computation.1 | convolution fusion | flops 1886380032 | bytes 17072128 | tf_op jit(solution)/shard_map/dot_general | solution.py:76
  58.9 0.1 broadcast_in_dim.12
  59.0 0.0 copy-start.1
  59.0 24.9 %all_to_all.23 = f32[32,1024,8]{1,2,0:T(8,128)S(1)} all-to-all(f32[32,1024,8]{1,2,0:T(8,128)S(1)} %broadcast_in_dim.12), channel_id=1, replica_groups=mesh['param_0'=8,'param_1'=4,'task_0'=4,'task_1'=2] {'param_1','task_0',..., dimensions={0} | all-to-all | bytes 2097152 | tf_op jit(solution)/shard_map/all_to_all | solution.py:23
  83.9 0.1 reduce_sum.28
  84.0 0.7 broadcast_in_dim.13
  84.7 3.4 %all-to-all-start.3 = ((f32[8,1024,8]{1,2,0:T(8,128)}), f32[8,1024,8]{1,2,0:T(8,128)S(1)}, u32[]{:S(2)}, u32[]{:S(2)}) async-start(f32[8,1024,8]{1,2,0:T(8,128)} %broadcast_in_dim.13), calls=%async_computation.3 | async-start | bytes 524288 | tf_op jit(solution)/shard_map/all_to_all | solution.py:23
  88.1 0.0 copy-done.1
  88.1 12.3 %all-to-all-done.3 = f32[8,1024,8]{1,2,0:T(8,128)S(1)} async-done(((f32[8,1024,8]{1,2,0:T(8,128)}), f32[8,1024,8]{1,2,0:T(8,128)S(1)}, u32[]{:S(2)}, u32[]{:S(2)}) %all-to-all-start.3) | async-done | bytes 262176 | tf_op jit(solution)/shard_map/all_to_all | solution.py:23
  100.4 9.7 %multiply_convert_fusion = bf16[1024,8,448]{0,2,1:T(8,128)(2,1)} fusion(f32[1024,8,448]{0,2,1:T(8,128)} %get-tuple-element.6, f32[8,448]{1,0:T(8,128)S(1)} %convert_element_type.23, f32[1024,8]{0,1:T(8,128)S(1)} %add_rsqrt_fusion), kind=kLoop, calls=%fused_computation | loop fusion | flops 11010048 | bytes 22067200 | tf_op jit(solution)/shard_map/convert_element_type | solution.py:82
  (3 shorter events, 0.0 us)
Async XLA Ops:
  0.0 51.6 %copy-start = (bf16[256,8,448]{0,2,1:T(8,128)(2,1)S(1)}, bf16[256,8,448]{0,2,1:T(8,128)(2,1)}, u32[]{:S(2)}) copy-start(bf16[256,8,448]{0,2,1:T(8,128)(2,1)} %param.10) | copy-start | bytes 5505028
  49.0 1.5 %copy-start.2 = (bf16[512,256]{1,0:T(8,128)(2,1)S(1)}, bf16[512,256]{1,0:T(8,128)(2,1)}, u32[]{:S(2)}) copy-start(bf16[512,256]{1,0:T(8,128)(2,1)} %param.9) | copy-start | bytes 786436
  49.0 1.5 %copy-start.3 = (bf16[256,512]{1,0:T(8,128)(2,1)S(1)}, bf16[256,512]{1,0:T(8,128)(2,1)}, u32[]{:S(2)}) copy-start(bf16[256,512]{1,0:T(8,128)(2,1)} %param.8) | copy-start | bytes 786436
  59.0 29.1 %copy-start.1 = (bf16[8,448]{1,0:T(8,128)(2,1)S(1)}, bf16[8,448]{1,0:T(8,128)(2,1)}, u32[]{:S(2)}) copy-start(bf16[8,448]{1,0:T(8,128)(2,1)} %param.11) | copy-start | bytes 21508
  84.7 15.7 %all-to-all-start.3 = ((f32[8,1024,8]{1,2,0:T(8,128)}), f32[8,1024,8]{1,2,0:T(8,128)S(1)}, u32[]{:S(2)}, u32[]{:S(2)}) async-start(f32[8,1024,8]{1,2,0:T(8,128)} %broadcast_in_dim.13), calls=%async_computation.3 | async-start | bytes 524288 | tf_op jit(solution)/shard_map/all_to_all | solution.py:23
